TPU v7x, 32 devices: a whole 2x2x4 slice. The times are simulated.
32 devices in a mesh: member: 2 (over y), seq: 4 (over z), dp: 2 (over x), mp: 2 (over core).
Axes of the slice: x: 2, y: 2, z: 4, core: 2. Of those that a mesh axis runs over, the one named last changes fastest.
Arguments:
- mixer_in: bfloat16 [4, 512, 3072], P(('member', 'dp'), 'seq', 'mp'), parts along dimension 0, may hold values from -6 to 6
- delta_raw: bfloat16 [4, 512, 3072], P(('member', 'dp'), 'seq', 'mp'), parts along dimension 0, may hold values from -2 to 512
- delta_bias: float32 [6144], P(('member', 'mp')), parts along dimension 0, may hold values from -4 to -2
- decay_log: float32 [6144, 16], P(('member', 'mp')), parts along dimension 0, may hold values from -12 to 1
- skip_gain: float32 [6144], P(('member', 'mp')), parts along dimension 0, may hold values from 0.5 to 1.5
- state_write: bfloat16 [4, 512, 16], P(('member', 'dp'), 'seq'), parts along dimension 0, may hold values from -5 to 5
- state_read: bfloat16 [4, 512, 16], P(('member', 'dp'), 'seq'), parts along dimension 0, may hold values from -1.5 to 1.5
- mixer_grad: bfloat16 [4, 512, 3072], P(('member', 'dp'), 'seq', 'mp'), parts along dimension 0, may hold values from -6 to 6
- attn_query: bfloat16 [4, 512, 1536], P(('member', 'dp'), 'seq', 'mp'), parts along dimension 0, may hold values from -5 to 5
- attn_key: bfloat16 [4, 512, 1536], P(('member', 'dp'), 'seq', 'mp'), parts along dimension 0, may hold values from -5 to 5
- attn_value: bfloat16 [4, 512, 1536], P(('member', 'dp'), 'seq', 'mp'), parts along dimension 0, may hold values from -6 to 6
- attn_grad: bfloat16 [4, 512, 1536], P(('member', 'dp'), 'seq', 'mp'), parts along dimension 0, may hold values from -6 to 6
- document_id: int32 [4, 512], P(('member', 'dp'), 'seq'), parts along dimension 0, may hold values from 0 to 3, never falling along the last dimension, each value on 1 to 256 neighbouring positions
Outputs:
- mixer_out: bfloat16 [4, 512, 3072], P(('member', 'dp'), 'seq', 'mp'), parts along dimension 0
- input_grad: bfloat16 [4, 512, 3072], P(('member', 'dp'), 'seq', 'mp'), parts along dimension 0
- delta_grad: bfloat16 [4, 512, 3072], P(('member', 'dp'), 'seq', 'mp'), parts along dimension 0
- decay_grad: float32 [6144, 16], P(('member', 'mp')), parts along dimension 0
- skip_grad: float32 [6144], P(('member', 'mp')), parts along dimension 0
- bias_grad: float32 [6144], P(('member', 'mp')), parts along dimension 0
- attn_out: bfloat16 [4, 512, 1536], P(('member', 'dp'), 'seq', 'mp'), parts along dimension 0
- query_grad: bfloat16 [4, 512, 1536], P(('member', 'dp'), 'seq', 'mp'), parts along dimension 0
- key_grad: bfloat16 [4, 512, 1536], P(('member', 'dp'), 'seq', 'mp'), parts along dimension 0
- value_grad: bfloat16 [4, 512, 1536], P(('member', 'dp'), 'seq', 'mp'), parts along dimension 0
There are 2 independent parts, one for each index of `member`. A program takes and returns all parts, laid end to end along the dimension named above; each array names one. Nothing has to cross between parts.
Inputs may be any that keep to these rules, and one draw needn't show every extreme that they name: `document_id`: document numbers never fall along a sequence; a document covers at most 256 positions.
All inputs are finite; a program needn't handle non-finite values.
Results may differ from a plain program's by a relative error of at most 0.024.
Values may be sent and summed in bfloat16 or wider, within the bound.
A program may use at most 128 MiB of HBM per device.

v0:
```python
import math
import jax
import jax.numpy as jnp
from jax import lax
from jax.sharding import PartitionSpec as P

HD = 96
WINDOW = 128
neg_large = -1e30
unroll_steps = 8


def prefix_2(x, axis, combine, identity, reverse):
    count, position = (lax.axis_size(axis), lax.axis_index(axis))
    everything = jax.tree.map(lambda part: lax.all_gather(part, axis), x)
    start = jax.tree.map(
        lambda part, zero: jnp.broadcast_to(jnp.asarray(zero, part.dtype), part.shape), x, identity
    )

    def lap(k, before):
        at = count - 1 - k if reverse else k
        reached = at > position if reverse else at < position
        new = combine(before, jax.tree.map(lambda part: part[at], everything))
        return jax.tree.map(lambda a, b: jnp.where(reached, a, b), new, before)

    return lax.fori_loop(0, count, lap, start)


def shifted(value, axis, steps):
    count = lax.axis_size(axis)
    leading, last = (max(0, -steps), min(count, count - steps))
    return lax.ppermute(value, axis, [(source, source + steps) for source in range(leading, last)])


def compose(earlier, later):
    return (earlier[0] * later[0], later[1] + later[0] * earlier[1])


def summaries(step_size, weighted, writes, reads, grads, rate):
    prefix = jnp.cumsum(step_size, axis=0)
    total = prefix[-1]
    suffix = total[None, :] - prefix
    through = jnp.exp(rate * total[:, None])
    ending = jnp.sum(
        weighted[:, :, None] * writes[:, None, :] * jnp.exp(suffix[:, :, None] * rate[None]), axis=0
    )
    leading = jnp.sum(
        grads[:, :, None] * reads[:, None, :] * jnp.exp(prefix[:, :, None] * rate[None]), axis=0
    )
    return (through, ending, leading)


def run_forward(start, step_size, weighted, writes, rate):
    count = step_size.shape[0] // unroll_steps

    def advance(state, items):
        sizes, weights, write_rows = items
        outputs = []
        for position in range(unroll_steps):
            state = (
                jnp.exp(sizes[position][:, None] * rate) * state
                + weights[position][:, None] * write_rows[position][None, :]
            )
            outputs.append(state)
        return (state, jnp.stack(outputs))

    shaped = (
        step_size.reshape(count, unroll_steps, -1),
        weighted.reshape(count, unroll_steps, -1),
        writes.reshape(count, unroll_steps, -1),
    )
    _, states = lax.scan(advance, start, shaped)
    return states.reshape((count * unroll_steps,) + start.shape)


def run_backward(start, step_size, inputs, grads, writes, reads, previous, rate, skip_gain):
    count = step_size.shape[0] // unroll_steps
    channels = step_size.shape[1]

    def retreat(carry, items):
        back, accum = carry
        sizes, values, outs, write_rows, read_rows, prior = items
        input_list = []
        step_list = []
        for position in reversed(range(unroll_steps)):
            decay = jnp.exp(sizes[position][:, None] * rate)
            adjoint = read_rows[position][None, :] * outs[position][:, None] + back
            through_write = jnp.sum(adjoint * write_rows[position][None, :], axis=1)
            input_list.append(through_write * sizes[position] + skip_gain * outs[position])
            tail = adjoint * prior[position] * decay
            step_list.append(values[position] * through_write + jnp.sum(tail * rate, axis=1))
            accum = accum + tail * sizes[position][:, None]
            back = decay * adjoint
        return ((back, accum), (jnp.stack(input_list[::-1]), jnp.stack(step_list[::-1])))

    shaped = (
        step_size.reshape(count, unroll_steps, -1),
        inputs.reshape(count, unroll_steps, -1),
        grads.reshape(count, unroll_steps, -1),
        writes.reshape(count, unroll_steps, -1),
        reads.reshape(count, unroll_steps, -1),
        previous.reshape((count, unroll_steps) + start.shape),
    )
    (_, accum), (input_grad, step_grad) = lax.scan(
        retreat, (start, jnp.zeros_like(start)), shaped, reverse=True
    )
    return (input_grad.reshape(-1, channels), step_grad.reshape(-1, channels), accum)


def body(
    mixer_in,
    delta_raw,
    delta_bias,
    decay_log,
    skip_gain,
    state_write,
    state_read,
    mixer_grad,
    attn_query,
    attn_key,
    attn_value,
    attn_grad,
    document_id,
):
    inputs = mixer_in[0].astype(jnp.float32)
    raws = delta_raw[0].astype(jnp.float32)
    grads = mixer_grad[0].astype(jnp.float32)
    writes = state_write[0].astype(jnp.float32)
    reads = state_read[0].astype(jnp.float32)
    rate = -jnp.exp(decay_log)
    step_size = jax.nn.softplus(raws + delta_bias[None, :])
    weighted = step_size * inputs
    through, ending, leading = summaries(step_size, weighted, writes, reads, grads, rate)
    zeros = jnp.zeros_like(through)
    ones = jnp.ones_like(through)
    forward_pair = prefix_2((through, ending), "seq", compose, (ones, zeros), False)
    backward_pair = prefix_2((through, leading), "seq", compose, (ones, zeros), True)
    state_start = forward_pair[1]
    adjoint_start = backward_pair[1]
    states = run_forward(state_start, step_size, weighted, writes, rate)
    mixed = jnp.sum(states * reads[:, None, :], axis=2) + skip_gain[None, :] * inputs
    previous = jnp.concatenate([state_start[None], states[:-1]], axis=0)
    input_grad, step_grad, decay_part = run_backward(
        adjoint_start, step_size, inputs, grads, writes, reads, previous, rate, skip_gain
    )
    raw_grad = step_grad * jax.nn.sigmoid(raws + delta_bias[None, :])
    sums = lax.psum(
        (decay_part * rate, jnp.sum(grads * inputs, axis=0), jnp.sum(raw_grad, axis=0)),
        ("seq", "dp"),
    )
    grad_scale = 1.0 / math.sqrt(inputs.shape[0] * lax.axis_size("seq") * lax.axis_size("dp"))
    query = attn_query[0]
    key_now = attn_key[0]
    value_now = attn_value[0]
    out_grad = attn_grad[0]
    length = query.shape[0]
    width = query.shape[1]
    heads = width // HD
    doc_now = (document_id[0] + 1).astype(jnp.bfloat16)
    key_before, value_before, doc_before = shifted((key_now, value_now, doc_now), "seq", 1)
    key_all = jnp.concatenate([key_before, key_now], axis=0).reshape(2 * length, heads, HD)
    value_all = jnp.concatenate([value_before, value_now], axis=0).reshape(2 * length, heads, HD)
    doc_all = jnp.concatenate([doc_before, doc_now], axis=0)
    query_heads = query.reshape(length, heads, HD)
    grad_heads = out_grad.reshape(length, heads, HD)
    offset = jnp.arange(length)[:, None] + length - jnp.arange(2 * length)[None, :]
    allowed = (offset >= 0) & (offset < WINDOW) & (doc_all[None, :] == doc_now[:, None])
    scale = 1.0 / math.sqrt(HD)
    scores = (
        jnp.einsum("qhd,khd->hqk", query_heads, key_all, preferred_element_type=jnp.float32) * scale
    )
    scores = jnp.where(allowed[None], scores, neg_large)
    top = jnp.max(scores, axis=2)
    log_total = top + jnp.log(jnp.sum(jnp.exp(scores - top[:, :, None]), axis=2))
    probs = jnp.exp(scores - log_total[:, :, None])
    probs_low = probs.astype(jnp.bfloat16)
    attended = jnp.einsum(
        "hqk,khd->qhd", probs_low, value_all, preferred_element_type=jnp.float32
    ).astype(jnp.bfloat16)
    row_term = jnp.einsum("qhd,qhd->hq", grad_heads, attended, preferred_element_type=jnp.float32)
    value_score = jnp.einsum(
        "qhd,khd->hqk", grad_heads, value_all, preferred_element_type=jnp.float32
    )
    score_grad = (probs * (value_score - row_term[:, :, None])).astype(jnp.bfloat16)
    query_grad = (
        jnp.einsum("hqk,khd->qhd", score_grad, key_all, preferred_element_type=jnp.float32) * scale
    ).astype(jnp.bfloat16)
    own_key = (
        jnp.einsum(
            "hqk,qhd->khd",
            score_grad[:, :, length:],
            query_heads,
            preferred_element_type=jnp.float32,
        )
        * scale
    )
    own_value = jnp.einsum(
        "hqk,qhd->khd", probs_low[:, :, length:], grad_heads, preferred_element_type=jnp.float32
    )
    next_query, next_grad, next_doc = shifted((query, out_grad, doc_now), "seq", -1)
    next_total, next_term = shifted((log_total, row_term), "seq", -1)
    next_query_heads = next_query.reshape(length, heads, HD)
    next_grad_heads = next_grad.reshape(length, heads, HD)
    key_heads = key_now.reshape(length, heads, HD)
    value_heads = value_now.reshape(length, heads, HD)
    next_offset = jnp.arange(length)[:, None] + length - jnp.arange(length)[None, :]
    next_allowed = (next_offset < WINDOW) & (doc_now[None, :] == next_doc[:, None])
    next_scores = (
        jnp.einsum("qhd,khd->hqk", next_query_heads, key_heads, preferred_element_type=jnp.float32)
        * scale
    )
    next_scores = jnp.where(next_allowed[None], next_scores, neg_large)
    next_probs = jnp.exp(next_scores - next_total[:, :, None])
    next_value_score = jnp.einsum(
        "qhd,khd->hqk", next_grad_heads, value_heads, preferred_element_type=jnp.float32
    )
    next_score_grad = (next_probs * (next_value_score - next_term[:, :, None])).astype(jnp.bfloat16)
    key_total = (
        own_key
        + jnp.einsum(
            "hqk,qhd->khd", next_score_grad, next_query_heads, preferred_element_type=jnp.float32
        )
        * scale
    )
    value_total = own_value + jnp.einsum(
        "hqk,qhd->khd",
        next_probs.astype(jnp.bfloat16),
        next_grad_heads,
        preferred_element_type=jnp.float32,
    )
    key_total = key_total.reshape(length, width)
    value_total = value_total.reshape(length, width)
    return (
        mixed.astype(jnp.bfloat16)[None],
        input_grad.astype(jnp.bfloat16)[None],
        raw_grad.astype(jnp.bfloat16)[None],
        sums[0] * grad_scale,
        sums[1] * grad_scale,
        sums[2] * grad_scale,
        attended.reshape(length, width)[None],
        query_grad.reshape(length, width)[None],
        key_total.astype(jnp.bfloat16)[None],
        value_total.astype(jnp.bfloat16)[None],
    )


def solution(mesh):
    return jax.shard_map(
        body,
        mesh=mesh,
        in_specs=(
            P(("member", "dp"), "seq", "mp"),
            P(("member", "dp"), "seq", "mp"),
            P(("member", "mp")),
            P(("member", "mp"), None),
            P(("member", "mp")),
            P(("member", "dp"), "seq", None),
            P(("member", "dp"), "seq", None),
            P(("member", "dp"), "seq", "mp"),
            P(("member", "dp"), "seq", "mp"),
            P(("member", "dp"), "seq", "mp"),
            P(("member", "dp"), "seq", "mp"),
            P(("member", "dp"), "seq", "mp"),
            P(("member", "dp"), "seq"),
        ),
        out_specs=(
            P(("member", "dp"), "seq", "mp"),
            P(("member", "dp"), "seq", "mp"),
            P(("member", "dp"), "seq", "mp"),
            P(("member", "mp"), None),
            P(("member", "mp")),
            P(("member", "mp")),
            P(("member", "dp"), "seq", "mp"),
            P(("member", "dp"), "seq", "mp"),
            P(("member", "dp"), "seq", "mp"),
            P(("member", "dp"), "seq", "mp"),
        ),
        check_vma=False,
    )
```

profile of v0, /device:TPU:16, one launch (start us, length us, event | category | flops | bytes accessed | tf_op | source)
XLA Modules:
  0.0 438.5 jit_solution(15867463959212674364)
XLA Ops:
  8.5 3.5 collective-permute-start.1
  12.0 2.4 collective-permute-start.3
  14.3 2.7 convert_bitcast_fusion.4
  17.1 2.7 fusion.88
  19.8 1.6 fusion.133
  28.0 1.6 multiply_exponential_fusion.8
  30.3 7.0 %multiply_reduce_fusion.16 = (f32[1536,16]{0,1:T(8,128)}, f32[1536,16]{0,1:T(8,128)S(1)}) fusion(f32[128,1536]{1,0:T(8,128)S(1)} %reduce_window_sum.11, f32[128,16]{1,0:T(8,128)} %copy.78, f32[128,1536]{1,0:T(8,128)} %get-tuple-element.855, f32[1536,16]{0,1:T(8,128)S(1)} %get-tuple-element.1339, f32[128,1536]{1,0:T(8,128)S(1)} %broadcast_subtract_fusion, ...), kind=kLoop, calls=%fused_computation.226 | loop fusion | flops 25116672 | bytes 3457024 | tf_op jit(solution)/shard_map/reduce_sum | solution.py:47
  37.3 12.9 %all-gather = f32[6144,16]{0,1:T(8,128)S(1)} all-gather(f32[1536,16]{0,1:T(8,128)S(1)} %get-tuple-element.722), channel_id=2, replica_groups=mesh['member'=2,'seq'=4,'dp'=2,'mp'=2] {'seq'}, dimensions={0}, use_global_device_ids=true | all-gather | bytes 491520 | tf_op jit(solution)/shard_map/all_gather | solution.py:15
  50.5 15.7 %all-gather.1 = f32[6144,16]{0,1:T(8,128)S(1)} all-gather(f32[1536,16]{0,1:T(8,128)} %get-tuple-element.856), channel_id=3, replica_groups=mesh['member'=2,'seq'=4,'dp'=2,'mp'=2] {'seq'}, dimensions={0}, use_global_device_ids=true | all-gather | bytes 491520 | tf_op jit(solution)/shard_map/all_gather | solution.py:15
  67.0 43.8 %while.63 = (s32[]{:T(128)}, f32[1536,16]{0,1:T(8,128)S(1)}, f32[16,8,1536,16]{2,3,1,0:T(8,128)}, f32[16,8,1536]{2,1,0:T(8,128)S(1)}, f32[1536,16]{0,1:T(8,128)S...) while((s32[]{:T(128)}, f32[1536,16]{0,1:T(8,128)S(1)}, ...), condition=%wide.region_5.6_spmd, body=%wide.region_4.5_spmd.sunk | while | flops 1966088 | bytes 4661081 | solution.py:72
  110.8 14.3 %all-gather.2 = f32[6144,16]{0,1:T(8,128)S(1)} all-gather(f32[1536,16]{0,1:T(8,128)S(1)} %copy-done.11), channel_id=4, replica_groups=mesh['member'=2,'seq'=4,'dp'=2,'mp'=2] {'seq'}, dimensions={0}, use_global_device_ids=true | all-gather | bytes 491520 | tf_op jit(solution)/shard_map/all_gather | solution.py:15
  126.1 11.5 %slice.665 = f32[127,1536,16]{1,2,0:T(8,128)} slice(f32[128,1536,16]{1,2,0:T(8,128)} %bitcast.504), slice={[0:127], [0:1536], [0:16]} | slice | bytes 24969216 | tf_op jit(solution)/shard_map/slice | solution.py:142
  137.5 11.5 %pad_maximum_fusion = f32[128,1536,16]{1,2,0:T(8,128)} fusion(f32[127,1536,16]{1,2,0:T(8,128)} %slice.665, f32[1,1536,16]{1,2,0:T(8,128)S(1)} %bitcast.506), kind=kLoop, calls=%fused_computation.225 | loop fusion | flops 3145728 | bytes 25165824 | tf_op jit(solution)/shard_map/concatenate | solution.py:142
  149.2 190.1 %while.66 = (s32[]{:T(128)}, f32[1536,16]{0,1:T(8,128)S(1)}, f32[1536,16]{0,1:T(8,128)S(1)}, bf16[16,8,1536]{2,1,0:T(8,128)(2,1)}, f32[16,8,1536]{2,1,0:T(8,128)...) while((s32[]{:T(128)}, f32[1536,16]{0,1:T(8,128)S(1)}, ...), condition=%wide.region_27.28_spmd.clone, body=%wide.region_10.27_spmd.clone.sunk | while | flops 4374539 | bytes 4418103 | solution.py:104
  154.0 1.6 fusion.169
  161.1 1.5 fusion.168
  165.9 1.6 fusion.169
  172.9 1.5 fusion.168
  177.7 1.6 fusion.169
  189.6 1.6 fusion.169
  201.4 1.6 fusion.169
  213.3 1.6 fusion.169
  225.1 1.6 fusion.169
  236.9 1.6 fusion.169
  244.0 1.5 fusion.168
  248.8 1.6 fusion.169
  255.9 1.5 fusion.168
  260.7 1.6 fusion.169
  267.8 1.5 fusion.168
  272.5 1.6 fusion.169
  284.4 1.6 fusion.169
  296.3 1.6 fusion.169
  308.1 1.6 fusion.169
  315.2 1.7 fusion.168
  320.1 1.6 fusion.169
  323.0 1.5 fusion.170
  332.2 1.6 fusion.169
  340.0 5.4 %collective-permute-start.2 = (bf16[128,768]{1,0:T(8,128)(2,1)S(1)}, bf16[128,768]{1,0:T(8,128)(2,1)S(1)}, u32[]{:S(2)}, u32[]{:S(2)}) collective-permute-start(bf16[128,768]{1,0:T(8,128)(2,1)S(1)} %bitcast.530), channel_id=1, source_target_pairs={{0,4},{4,8},{8,12},{1,5},{5,9},{9,13},{2,6},{6,10},{10,14},{3,7},{... | collective-permute-start | bytes 589832 | tf_op jit(solution)/shard_map/ppermute | solution.py:32
  345.4 1.9 collective-permute-start
  347.3 4.1 collective-permute-start.4
  351.5 7.0 %multiply_reduce_fusion.17 = f32[16,8,1536]{2,1,0:T(8,128)S(1)} fusion(f32[16,8,1536,16]{2,3,1,0:T(8,128)} %get-tuple-element.531, f32[16,8,16]{2,1,0:T(8,128)S(1)} %get-tuple-element.1408), kind=kLoop, calls=%fused_computation.227 | loop fusion | flops 6094848 | bytes 13377536 | tf_op jit(solution)/shard_map/reduce_sum | solution.py:141
  360.5 30.6 %all-reduce = (f32[1536]{0:T(1024)S(1)}, f32[1536]{0:T(1024)S(1)}) all-reduce(f32[1536]{0:T(1024)S(1)} %get-tuple-element.853, f32[1536]{0:T(1024)S(1)} %fusion.118), channel_id=1, replica_groups=mesh['member'=2,'seq'=4,'dp'=2,'mp'=2] {'seq','dp'}, use_global_device_ids=true, to_apply=%region_30.31 | all-reduce | flops 3072 | bytes 24576 | tf_op jit(solution)/shard_map/psum | solution.py:147
  393.1 5.2 %collective-permute-start.6 = (bf16[128,768]{1,0:T(8,128)(2,1)S(1)}, bf16[128,768]{1,0:T(8,128)(2,1)}, u32[]{:S(2)}, u32[]{:S(2)}) collective-permute-start(bf16[128,768]{1,0:T(8,128)(2,1)S(1)} %bitcast.533), channel_id=1, source_target_pairs={{4,0},{8,4},{12,8},{5,1},{9,5},{13,9},{6,2},{10,6},{14,10},{7,3},{... | collective-permute-start | bytes 589832 | tf_op jit(solution)/shard_map/ppermute | solution.py:32
  400.5 11.9 %all-reduce.3.cloned.1.call-done = f32[1536,16]{0,1:T(8,128)} async-done(((f32[1536,16]{0,1:T(8,128)}), f32[1536,16]{0,1:T(8,128)}) %all-reduce.3.cloned.1.call-update) | async-done | bytes 98320 | tf_op jit(solution)/shard_map/psum | solution.py:147
  412.4 1.5 broadcast_multiply_fusion
  414.7 2.7 collective-permute-start.5
  418.7 3.1 collective-permute-start.7
  425.4 1.7 copy.93
  (546 shorter events, 224.9 us)
Async XLA Ops:
  7.2 405.2 %all-reduce.3.cloned.1.call-start = ((), (), s32[]{:S(2)}) async-start(), calls=%async_computation | async-start | bytes 196608 | tf_op jit(solution)/shard_map/psum | solution.py:147
  8.5 384.6 %collective-permute-start.1 = (bf16[128]{0:T(256)(128)(2,1)}, bf16[128]{0:T(256)(128)(2,1)}, u32[]{:S(2)}, u32[]{:S(2)}) collective-permute-start(bf16[128]{0:T(256)(128)(2,1)} %convert_bitcast_fusion.9), channel_id=1, source_target_pairs={{0,4},{4,8},{8,12},{1,5},{5,9},{9,13},{2,6},{6,10},{10,14},{3,7},{... | collective-permute-start | bytes 776 | tf_op jit(solution)/shard_map/ppermute | solution.py:32
  12.0 387.8 %collective-permute-start.3 = (bf16[128]{0:T(256)(128)(2,1)}, bf16[128]{0:T(256)(128)(2,1)}, u32[]{:S(2)}, u32[]{:S(2)}) collective-permute-start(bf16[128]{0:T(256)(128)(2,1)} %convert_bitcast_fusion.9), channel_id=1, source_target_pairs={{4,0},{8,4},{12,8},{5,1},{9,5},{13,9},{6,2},{10,6},{14,10},{7,3},{... | collective-permute-start | bytes 776 | tf_op jit(solution)/shard_map/ppermute | solution.py:32
  66.9 43.8 %copy-start.11 = (f32[1536,16]{0,1:T(8,128)S(1)}, f32[1536,16]{0,1:T(8,128)}, u32[]{:S(2)}) copy-start(f32[1536,16]{0,1:T(8,128)} %get-tuple-element.721) | copy-start | bytes 294916
  137.5 11.6 %copy-start.3 = (f32[1,128,16]{2,1,0:T(8,128)S(1)}, f32[1,128,16]{2,1,0:T(8,128)}, u32[]{:S(2)}) copy-start(f32[1,128,16]{2,1,0:T(8,128)} %copy.77) | copy-start | bytes 24580
  137.5 11.6 %copy-start.4 = (f32[1536]{0:T(1024)S(1)}, f32[1536]{0:T(1024)}, u32[]{:S(2)}) copy-start(f32[1536]{0:T(1024)} %param.25) | copy-start | bytes 18436
  149.2 190.2 %copy-start.2 = (f32[1536,16]{0,1:T(8,128)S(1)}, f32[1536,16]{0,1:T(8,128)}, u32[]{:S(2)}) copy-start(f32[1536,16]{0,1:T(8,128)} %param.24) | copy-start | bytes 294916
  149.2 190.8 %copy-start.5 = (bf16[1,128,768]{2,1,0:T(8,128)(2,1)S(1)}, bf16[1,128,768]{2,1,0:T(8,128)(2,1)}, u32[]{:S(2)}) copy-start(bf16[1,128,768]{2,1,0:T(8,128)(2,1)} %param.30) | copy-start | bytes 589828
  149.2 196.2 %copy-start.6 = (bf16[1,128,768]{2,1,0:T(8,128)(2,1)S(1)}, bf16[1,128,768]{2,1,0:T(8,128)(2,1)}, u32[]{:S(2)}) copy-start(bf16[1,128,768]{2,1,0:T(8,128)(2,1)} %param.31) | copy-start | bytes 589828
  149.2 198.1 %copy-start.7 = (bf16[1,128,768]{2,1,0:T(8,128)(2,1)S(1)}, bf16[1,128,768]{2,1,0:T(8,128)(2,1)}, u32[]{:S(2)}) copy-start(bf16[1,128,768]{2,1,0:T(8,128)(2,1)} %param.29) | copy-start | bytes 589828
  339.3 19.2 %copy-start.1 = (bf16[1,128,1536]{2,1,0:T(8,128)(2,1)S(1)}, bf16[1,128,1536]{2,1,0:T(8,128)(2,1)}, u32[]{:S(2)}) copy-start(bf16[1,128,1536]{2,1,0:T(8,128)(2,1)} %param.22) | copy-start | bytes 1179652
  339.3 19.2 %copy-start.10 = (f32[1536]{0:T(1024)S(1)}, f32[1536]{0:T(1024)}, u32[]{:S(2)}) copy-start(f32[1536]{0:T(1024)} %param.23) | copy-start | bytes 18436
  339.3 20.4 %copy-start = (bf16[1,128,1536]{2,1,0:T(8,128)(2,1)S(1)}, bf16[1,128,1536]{2,1,0:T(8,128)(2,1)}, u32[]{:S(2)}) copy-start(bf16[1,128,1536]{2,1,0:T(8,128)(2,1)} %param.21) | copy-start | bytes 1179652
  339.3 53.6 %copy-start.8 = (bf16[1,128,768]{2,1,0:T(8,128)(2,1)S(1)}, bf16[1,128,768]{2,1,0:T(8,128)(2,1)}, u32[]{:S(2)}) copy-start(bf16[1,128,768]{2,1,0:T(8,128)(2,1)} %param.32) | copy-start | bytes 589828
  340.0 73.9 %collective-permute-start.2 = (bf16[128,768]{1,0:T(8,128)(2,1)S(1)}, bf16[128,768]{1,0:T(8,128)(2,1)S(1)}, u32[]{:S(2)}, u32[]{:S(2)}) collective-permute-start(bf16[128,768]{1,0:T(8,128)(2,1)S(1)} %bitcast.530), channel_id=1, source_target_pairs={{0,4},{4,8},{8,12},{1,5},{5,9},{9,13},{2,6},{6,10},{10,14},{3,7},{... | collective-permute-start | bytes 589832 | tf_op jit(solution)/shard_map/ppermute | solution.py:32
  345.4 72.2 %collective-permute-start = (bf16[128,768]{1,0:T(8,128)(2,1)S(1)}, bf16[128,768]{1,0:T(8,128)(2,1)S(1)}, u32[]{:S(2)}, u32[]{:S(2)}) collective-permute-start(bf16[128,768]{1,0:T(8,128)(2,1)S(1)} %bitcast.531), channel_id=1, source_target_pairs={{0,4},{4,8},{8,12},{1,5},{5,9},{9,13},{2,6},{6,10},{10,14},{3,7},{... | collective-permute-start | bytes 589832 | tf_op jit(solution)/shard_map/ppermute | solution.py:32
  347.3 75.4 %collective-permute-start.4 = (bf16[128,768]{1,0:T(8,128)(2,1)S(1)}, bf16[128,768]{1,0:T(8,128)(2,1)}, u32[]{:S(2)}, u32[]{:S(2)}) collective-permute-start(bf16[128,768]{1,0:T(8,128)(2,1)S(1)} %bitcast.532), channel_id=1, source_target_pairs={{4,0},{8,4},{12,8},{5,1},{9,5},{13,9},{6,2},{10,6},{14,10},{7,3},{... | collective-permute-start | bytes 589832 | tf_op jit(solution)/shard_map/ppermute | solution.py:32
  393.1 34.8 %collective-permute-start.6 = (bf16[128,768]{1,0:T(8,128)(2,1)S(1)}, bf16[128,768]{1,0:T(8,128)(2,1)}, u32[]{:S(2)}, u32[]{:S(2)}) collective-permute-start(bf16[128,768]{1,0:T(8,128)(2,1)S(1)} %bitcast.533), channel_id=1, source_target_pairs={{4,0},{8,4},{12,8},{5,1},{9,5},{13,9},{6,2},{10,6},{14,10},{7,3},{... | collective-permute-start | bytes 589832 | tf_op jit(solution)/shard_map/ppermute | solution.py:32
  414.1 3.5 copy-start.9
  414.7 14.3 %collective-permute-start.5 = (f32[8,128]{1,0:T(8,128)S(1)}, f32[8,128]{1,0:T(8,128)S(1)}, u32[]{:S(2)}, u32[]{:S(2)}) collective-permute-start(f32[8,128]{1,0:T(8,128)S(1)} %log_add_fusion), channel_id=1, source_target_pairs={{4,0},{8,4},{12,8},{5,1},{9,5},{13,9},{6,2},{10,6},{14,10},{7,3},{... | collective-permute-start | bytes 12296 | tf_op jit(solution)/shard_map/ppermute | solution.py:32
  418.7 10.3 %collective-permute-start.7 = (f32[8,128]{1,0:T(8,128)S(1)}, f32[8,128]{1,0:T(8,128)S(1)}, u32[]{:S(2)}, u32[]{:S(2)}) collective-permute-start(f32[8,128]{1,0:T(8,128)S(1)} %get-tuple-element.860), channel_id=1, source_target_pairs={{4,0},{8,4},{12,8},{5,1},{9,5},{13,9},{6,2},{10,6},{14,10},{7,3},{... | collective-permute-start | bytes 12296 | tf_op jit(solution)/shard_map/ppermute | solution.py:32
Sparse Core Ops, SparseCore 0:
  340.1 72.2 all-reduce.2
where the time goes:
time: 447 us; the launch traced here: 439 us
  other arithmetic  200 us (45%)
  local copies, waits for them, and re-layouts  104 us (23%)
  blocking collectives  73.6 us (16%)
  starting transfers between devices  28.2 us (6%)
  between operations  14.5 us (3%)
  waiting for transfers between devices  11.9 us (3%)
  matrix products  4.72 us (1%)
    all_gather x3, blocking collectives, prefix_2(): everything = jax.tree.map(lambda part: lax.all_gather(part, axis), x)  42.9 us
    reduce_sum x32, other arithmetic, retreat(): jnp.sum(tail * rate, axis=1)  39.1 us
    add x32, other arithmetic, retreat(): values[position] * through_write + jnp.sum(tail * rate, axis=1)  32.7 us
    psum x1, blocking collectives, body(): lax.psum((decay_part * rate, jnp.sum(grads * inputs, axis=0), jnp.sum(raw...  30.6 us
    ppermute x8, starting transfers between devices, shifted(): lax.ppermute(value, axis, [(source, source + steps) for source in range(l...  28.2 us
    add x16, other arithmetic, retreat(): accum = accum + tail * sizes[position][:, None]  25 us
    slice x16, local copies, waits for them, and re-layouts, retreat(): adjoint = read_rows[position][None, :] * outs[position][:, None] + back  24.2 us
    dynamic_slice x32, local copies, waits for them, and re-layouts, run_forward(): _, states = lax.scan(advance, start, shaped)  22.2 us
  transfers between devices with their start and end apart: 9, of which 1 were waited for; matrix products, arithmetic and copies ran while one was open for 69% of the time, Pallas kernels for 0%

commit v1 on v0

--- a/solution.py
+++ b/solution.py
@@ -144,10 +144,9 @@
         adjoint_start, step_size, inputs, grads, writes, reads, previous, rate, skip_gain
     )
     raw_grad = step_grad * jax.nn.sigmoid(raws + delta_bias[None, :])
-    sums = lax.psum(
-        (decay_part * rate, jnp.sum(grads * inputs, axis=0), jnp.sum(raw_grad, axis=0)),
-        ("seq", "dp"),
-    )
+    sums = (decay_part * rate, jnp.sum(grads * inputs, axis=0), jnp.sum(raw_grad, axis=0))
+    for mesh_axis in ("dp", "seq"):
+        sums = lax.psum(sums, mesh_axis)
     grad_scale = 1.0 / math.sqrt(inputs.shape[0] * lax.axis_size("seq") * lax.axis_size("dp"))
     query = attn_query[0]
     key_now = attn_key[0]

time: 447 us -> 452 us (1.011)
  the two profiles are of different devices: /device:TPU:16 before, /device:TPU:0 now
where the time goes in v1:
time: 452 us; the launch traced here: 444 us
  other arithmetic  200 us (44%)
  local copies, waits for them, and re-layouts  104 us (23%)
  blocking collectives  74 us (16%)
  waiting for transfers between devices  27.1 us (6%)
  starting transfers between devices  17.6 us (4%)
  between operations  14.6 us (3%)
  matrix products  4.72 us (1%)
    all_gather x3, blocking collectives, prefix_2(): everything = jax.tree.map(lambda part: lax.all_gather(part, axis), x)  45.4 us
    reduce_sum x32, other arithmetic, retreat(): jnp.sum(tail * rate, axis=1)  39.1 us
    add x32, other arithmetic, retreat(): values[position] * through_write + jnp.sum(tail * rate, axis=1)  32.7 us
    psum x2, blocking collectives, body(): sums = lax.psum(sums, mesh_axis)  28.6 us
    psum x2, waiting for transfers between devices, body(): sums = lax.psum(sums, mesh_axis)  27 us
    add x16, other arithmetic, retreat(): accum = accum + tail * sizes[position][:, None]  25 us
    slice x16, local copies, waits for them, and re-layouts, retreat(): adjoint = read_rows[position][None, :] * outs[position][:, None] + back  24.2 us
    dynamic_slice x32, local copies, waits for them, and re-layouts, run_forward(): _, states = lax.scan(advance, start, shaped)  22.2 us
  transfers between devices with their start and end apart: 10, of which 1 were waited for; matrix products, arithmetic and copies ran while one was open for 69% of the time, Pallas kernels for 0%

profile of v1, /device:TPU:0, one launch (start us, length us, event | category | flops | bytes accessed | tf_op | source)
XLA Modules:
  0.0 443.5 jit_solution(8906442803298692925)
XLA Ops:
  8.5 5.5 %collective-permute-start.1 = (bf16[128]{0:T(256)(128)(2,1)}, bf16[128]{0:T(256)(128)(2,1)}, u32[]{:S(2)}, u32[]{:S(2)}) collective-permute-start(bf16[128]{0:T(256)(128)(2,1)} %convert_bitcast_fusion.9), channel_id=1, source_target_pairs={{0,4},{4,8},{8,12},{1,5},{5,9},{9,13},{2,6},{6,10},{10,14},{3,7},{... | collective-permute-start | bytes 776 | tf_op jit(solution)/shard_map/ppermute | solution.py:32
  15.2 2.7 convert_bitcast_fusion.4
  18.0 2.7 fusion.88
  20.7 1.6 fusion.133
  28.9 1.6 multiply_exponential_fusion.8
  31.2 7.0 %multiply_reduce_fusion.16 = (f32[1536,16]{0,1:T(8,128)}, f32[1536,16]{0,1:T(8,128)S(1)}) fusion(f32[128,1536]{1,0:T(8,128)S(1)} %reduce_window_sum.11, f32[128,16]{1,0:T(8,128)} %copy.78, f32[128,1536]{1,0:T(8,128)} %get-tuple-element.857, f32[1536,16]{0,1:T(8,128)S(1)} %get-tuple-element.1341, f32[128,1536]{1,0:T(8,128)S(1)} %broadcast_subtract_fusion, ...), kind=kLoop, calls=%fused_computation.226 | loop fusion | flops 25116672 | bytes 3457024 | tf_op jit(solution)/shard_map/reduce_sum | solution.py:47
  38.2 15.5 %all-gather = f32[6144,16]{0,1:T(8,128)S(1)} all-gather(f32[1536,16]{0,1:T(8,128)S(1)} %get-tuple-element.722), channel_id=2, replica_groups=mesh['member'=2,'seq'=4,'dp'=2,'mp'=2] {'seq'}, dimensions={0}, use_global_device_ids=true | all-gather | bytes 491520 | tf_op jit(solution)/shard_map/all_gather | solution.py:15
  54.0 15.6 %all-gather.1 = f32[6144,16]{0,1:T(8,128)S(1)} all-gather(f32[1536,16]{0,1:T(8,128)} %get-tuple-element.858), channel_id=3, replica_groups=mesh['member'=2,'seq'=4,'dp'=2,'mp'=2] {'seq'}, dimensions={0}, use_global_device_ids=true | all-gather | bytes 491520 | tf_op jit(solution)/shard_map/all_gather | solution.py:15
  70.3 43.8 %while.63 = (s32[]{:T(128)}, f32[1536,16]{0,1:T(8,128)S(1)}, f32[16,8,1536,16]{2,3,1,0:T(8,128)}, f32[16,8,1536]{2,1,0:T(8,128)S(1)}, f32[1536,16]{0,1:T(8,128)S...) while((s32[]{:T(128)}, f32[1536,16]{0,1:T(8,128)S(1)}, ...), condition=%wide.region_5.6_spmd, body=%wide.region_4.5_spmd.sunk | while | flops 1966088 | bytes 4661081 | solution.py:72
  114.1 14.3 %all-gather.2 = f32[6144,16]{0,1:T(8,128)S(1)} all-gather(f32[1536,16]{0,1:T(8,128)S(1)} %copy-done.11), channel_id=4, replica_groups=mesh['member'=2,'seq'=4,'dp'=2,'mp'=2] {'seq'}, dimensions={0}, use_global_device_ids=true | all-gather | bytes 491520 | tf_op jit(solution)/shard_map/all_gather | solution.py:15
  129.4 11.5 %slice.665 = f32[127,1536,16]{1,2,0:T(8,128)} slice(f32[128,1536,16]{1,2,0:T(8,128)} %bitcast.504), slice={[0:127], [0:1536], [0:16]} | slice | bytes 24969216 | tf_op jit(solution)/shard_map/slice | solution.py:142
  140.9 11.5 %pad_maximum_fusion = f32[128,1536,16]{1,2,0:T(8,128)} fusion(f32[127,1536,16]{1,2,0:T(8,128)} %slice.665, f32[1,1536,16]{1,2,0:T(8,128)S(1)} %bitcast.506), kind=kLoop, calls=%fused_computation.225 | loop fusion | flops 3145728 | bytes 25165824 | tf_op jit(solution)/shard_map/concatenate | solution.py:142
  152.6 190.1 %while.66 = (s32[]{:T(128)}, f32[1536,16]{0,1:T(8,128)S(1)}, f32[1536,16]{0,1:T(8,128)S(1)}, bf16[16,8,1536]{2,1,0:T(8,128)(2,1)}, f32[16,8,1536]{2,1,0:T(8,128)...) while((s32[]{:T(128)}, f32[1536,16]{0,1:T(8,128)S(1)}, ...), condition=%wide.region_27.28_spmd.clone, body=%wide.region_10.27_spmd.clone.sunk | while | flops 4374539 | bytes 4418103 | solution.py:104
  157.4 1.6 fusion.169
  164.4 1.5 fusion.168
  169.2 1.6 fusion.169
  176.3 1.5 fusion.168
  181.1 1.6 fusion.169
  192.9 1.6 fusion.169
  204.8 1.6 fusion.169
  216.6 1.6 fusion.169
  228.5 1.6 fusion.169
  235.5 1.5 fusion.168
  240.3 1.6 fusion.169
  247.4 1.5 fusion.168
  252.2 1.6 fusion.169
  259.2 1.5 fusion.168
  264.0 1.6 fusion.169
  271.1 1.5 fusion.168
  275.9 1.6 fusion.169
  283.0 1.5 fusion.168
  287.8 1.6 fusion.169
  294.8 1.5 fusion.168
  299.6 1.6 fusion.169
  311.5 1.6 fusion.169
  318.5 1.7 fusion.168
  323.5 1.6 fusion.169
  326.3 1.5 fusion.170
  330.8 1.5 fusion.168
  335.6 1.6 fusion.169
  343.4 3.6 collective-permute-start.2
  347.0 1.9 collective-permute-start
  350.5 7.0 %multiply_reduce_fusion.17 = f32[16,8,1536]{2,1,0:T(8,128)S(1)} fusion(f32[16,8,1536,16]{2,3,1,0:T(8,128)} %get-tuple-element.531, f32[16,8,16]{2,1,0:T(8,128)S(1)} %get-tuple-element.1411), kind=kLoop, calls=%fused_computation.227 | loop fusion | flops 6094848 | bytes 13377536 | tf_op jit(solution)/shard_map/reduce_sum | solution.py:141
  359.5 8.1 %all-reduce.1 = (f32[1536]{0:T(1024)S(1)}, f32[1536]{0:T(1024)S(1)}) all-reduce(f32[1536]{0:T(1024)S(1)} %get-tuple-element.855, f32[1536]{0:T(1024)S(1)} %fusion.118), channel_id=1, replica_groups=mesh['member'=2,'seq'=4,'dp'=2,'mp'=2] {'dp'}, use_global_device_ids=true, to_apply=%region_31.32 | all-reduce | flops 3072 | bytes 24576 | tf_op jit(solution)/shard_map/psum | solution.py:149
  367.6 20.5 %all-reduce = (f32[1536]{0:T(1024)S(1)}, f32[1536]{0:T(1024)S(1)}) all-reduce(f32[1536]{0:T(1024)S(1)} %get-tuple-element.785, f32[1536]{0:T(1024)S(1)} %get-tuple-element.786), channel_id=1, replica_groups=mesh['member'=2,'seq'=4,'dp'=2,'mp'=2] {'seq'}, use_global_device_ids=true, to_apply=%region_32.33 | all-reduce | flops 3072 | bytes 24576 | tf_op jit(solution)/shard_map/psum | solution.py:149
  400.6 27.0 %all-reduce.7.cloned.1.call-done = f32[1536,16]{0,1:T(8,128)} async-done(((f32[1536,16]{0,1:T(8,128)}), f32[1536,16]{0,1:T(8,128)}) %all-reduce.7.cloned.1.call-update) | async-done | bytes 98320 | tf_op jit(solution)/shard_map/psum | solution.py:149
  427.6 1.5 broadcast_multiply_fusion
  430.3 1.7 copy.93
  (550 shorter events, 225.6 us)
Async XLA Ops:
  7.2 386.4 %all-reduce.5.cloned.1.call-start = ((), (), s32[]{:S(2)}) async-start(), calls=%async_computation | async-start | bytes 196608 | tf_op jit(solution)/shard_map/psum | solution.py:149
  8.5 381.5 %collective-permute-start.1 = (bf16[128]{0:T(256)(128)(2,1)}, bf16[128]{0:T(256)(128)(2,1)}, u32[]{:S(2)}, u32[]{:S(2)}) collective-permute-start(bf16[128]{0:T(256)(128)(2,1)} %convert_bitcast_fusion.9), channel_id=1, source_target_pairs={{0,4},{4,8},{8,12},{1,5},{5,9},{9,13},{2,6},{6,10},{10,14},{3,7},{... | collective-permute-start | bytes 776 | tf_op jit(solution)/shard_map/ppermute | solution.py:32
  13.9 378.8 %collective-permute-start.3 = (bf16[128]{0:T(256)(128)(2,1)}, bf16[128]{0:T(256)(128)(2,1)}, u32[]{:S(2)}, u32[]{:S(2)}) collective-permute-start(bf16[128]{0:T(256)(128)(2,1)} %convert_bitcast_fusion.9), channel_id=1, source_target_pairs={{4,0},{8,4},{12,8},{5,1},{9,5},{13,9},{6,2},{10,6},{14,10},{7,3},{... | collective-permute-start | bytes 776 | tf_op jit(solution)/shard_map/ppermute | solution.py:32
  70.3 43.8 %copy-start.11 = (f32[1536,16]{0,1:T(8,128)S(1)}, f32[1536,16]{0,1:T(8,128)}, u32[]{:S(2)}) copy-start(f32[1536,16]{0,1:T(8,128)} %get-tuple-element.721) | copy-start | bytes 294916
  140.9 11.6 %copy-start.3 = (f32[1,128,16]{2,1,0:T(8,128)S(1)}, f32[1,128,16]{2,1,0:T(8,128)}, u32[]{:S(2)}) copy-start(f32[1,128,16]{2,1,0:T(8,128)} %copy.77) | copy-start | bytes 24580
  140.9 11.6 %copy-start.4 = (f32[1536]{0:T(1024)S(1)}, f32[1536]{0:T(1024)}, u32[]{:S(2)}) copy-start(f32[1536]{0:T(1024)} %param.25) | copy-start | bytes 18436
  152.5 190.2 %copy-start.2 = (f32[1536,16]{0,1:T(8,128)S(1)}, f32[1536,16]{0,1:T(8,128)}, u32[]{:S(2)}) copy-start(f32[1536,16]{0,1:T(8,128)} %param.24) | copy-start | bytes 294916
  152.5 190.9 %copy-start.5 = (bf16[1,128,768]{2,1,0:T(8,128)(2,1)S(1)}, bf16[1,128,768]{2,1,0:T(8,128)(2,1)}, u32[]{:S(2)}) copy-start(bf16[1,128,768]{2,1,0:T(8,128)(2,1)} %param.30) | copy-start | bytes 589828
  152.6 194.5 %copy-start.6 = (bf16[1,128,768]{2,1,0:T(8,128)(2,1)S(1)}, bf16[1,128,768]{2,1,0:T(8,128)(2,1)}, u32[]{:S(2)}) copy-start(bf16[1,128,768]{2,1,0:T(8,128)(2,1)} %param.31) | copy-start | bytes 589828
  152.6 196.4 %copy-start.7 = (bf16[1,128,768]{2,1,0:T(8,128)(2,1)S(1)}, bf16[1,128,768]{2,1,0:T(8,128)(2,1)}, u32[]{:S(2)}) copy-start(bf16[1,128,768]{2,1,0:T(8,128)(2,1)} %param.29) | copy-start | bytes 589828
  342.6 14.8 %copy-start.1 = (bf16[1,128,1536]{2,1,0:T(8,128)(2,1)S(1)}, bf16[1,128,1536]{2,1,0:T(8,128)(2,1)}, u32[]{:S(2)}) copy-start(bf16[1,128,1536]{2,1,0:T(8,128)(2,1)} %param.22) | copy-start | bytes 1179652
  342.6 14.8 %copy-start.10 = (f32[1536]{0:T(1024)S(1)}, f32[1536]{0:T(1024)}, u32[]{:S(2)}) copy-start(f32[1536]{0:T(1024)} %param.23) | copy-start | bytes 18436
  342.7 16.0 %copy-start = (bf16[1,128,1536]{2,1,0:T(8,128)(2,1)S(1)}, bf16[1,128,1536]{2,1,0:T(8,128)(2,1)}, u32[]{:S(2)}) copy-start(bf16[1,128,1536]{2,1,0:T(8,128)(2,1)} %param.21) | copy-start | bytes 1179652
  342.7 47.1 %copy-start.8 = (bf16[1,128,768]{2,1,0:T(8,128)(2,1)S(1)}, bf16[1,128,768]{2,1,0:T(8,128)(2,1)}, u32[]{:S(2)}) copy-start(bf16[1,128,768]{2,1,0:T(8,128)(2,1)} %param.32) | copy-start | bytes 589828
  343.4 84.2 %all-reduce.7.cloned.1.call-start = ((), (), s32[]{:S(2)}) async-start(), calls=%async_computation.1 | async-start | bytes 196608 | tf_op jit(solution)/shard_map/psum | solution.py:149
  343.4 50.2 %collective-permute-start.2 = (bf16[128,768]{1,0:T(8,128)(2,1)S(1)}, bf16[128,768]{1,0:T(8,128)(2,1)S(1)}, u32[]{:S(2)}, u32[]{:S(2)}) collective-permute-start(bf16[128,768]{1,0:T(8,128)(2,1)S(1)} %bitcast.530), channel_id=1, source_target_pairs={{0,4},{4,8},{8,12},{1,5},{5,9},{9,13},{2,6},{6,10},{10,14},{3,7},{... | collective-permute-start | bytes 589832 | tf_op jit(solution)/shard_map/ppermute | solution.py:32
  347.0 48.8 %collective-permute-start = (bf16[128,768]{1,0:T(8,128)(2,1)S(1)}, bf16[128,768]{1,0:T(8,128)(2,1)S(1)}, u32[]{:S(2)}, u32[]{:S(2)}) collective-permute-start(bf16[128,768]{1,0:T(8,128)(2,1)S(1)} %bitcast.531), channel_id=1, source_target_pairs={{0,4},{4,8},{8,12},{1,5},{5,9},{9,13},{2,6},{6,10},{10,14},{3,7},{... | collective-permute-start | bytes 589832 | tf_op jit(solution)/shard_map/ppermute | solution.py:32
  349.0 49.9 %collective-permute-start.4 = (bf16[128,768]{1,0:T(8,128)(2,1)S(1)}, bf16[128,768]{1,0:T(8,128)(2,1)}, u32[]{:S(2)}, u32[]{:S(2)}) collective-permute-start(bf16[128,768]{1,0:T(8,128)(2,1)S(1)} %bitcast.532), channel_id=1, source_target_pairs={{4,0},{8,4},{12,8},{5,1},{9,5},{13,9},{6,2},{10,6},{14,10},{7,3},{... | collective-permute-start | bytes 589832 | tf_op jit(solution)/shard_map/ppermute | solution.py:32
  390.0 42.9 %collective-permute-start.6 = (bf16[128,768]{1,0:T(8,128)(2,1)S(1)}, bf16[128,768]{1,0:T(8,128)(2,1)}, u32[]{:S(2)}, u32[]{:S(2)}) collective-permute-start(bf16[128,768]{1,0:T(8,128)(2,1)S(1)} %bitcast.533), channel_id=1, source_target_pairs={{4,0},{8,4},{12,8},{5,1},{9,5},{13,9},{6,2},{10,6},{14,10},{7,3},{... | collective-permute-start | bytes 589832 | tf_op jit(solution)/shard_map/ppermute | solution.py:32
  393.8 2.0 copy-start.9
  394.4 39.7 %collective-permute-start.5 = (f32[8,128]{1,0:T(8,128)S(1)}, f32[8,128]{1,0:T(8,128)S(1)}, u32[]{:S(2)}, u32[]{:S(2)}) collective-permute-start(f32[8,128]{1,0:T(8,128)S(1)} %log_add_fusion), channel_id=1, source_target_pairs={{4,0},{8,4},{12,8},{5,1},{9,5},{13,9},{6,2},{10,6},{14,10},{7,3},{... | collective-permute-start | bytes 12296 | tf_op jit(solution)/shard_map/ppermute | solution.py:32
  396.9 37.1 %collective-permute-start.7 = (f32[8,128]{1,0:T(8,128)S(1)}, f32[8,128]{1,0:T(8,128)S(1)}, u32[]{:S(2)}, u32[]{:S(2)}) collective-permute-start(f32[8,128]{1,0:T(8,128)S(1)} %get-tuple-element.862), channel_id=1, source_target_pairs={{4,0},{8,4},{12,8},{5,1},{9,5},{13,9},{6,2},{10,6},{14,10},{7,3},{... | collective-permute-start | bytes 12296 | tf_op jit(solution)/shard_map/ppermute | solution.py:32
Sparse Core Ops, SparseCore 0:
  343.5 22.3 all-reduce.4
  393.7 33.8 all-reduce.6
